TPU v7x, 256 devices: a whole 4x4x8 slice. The times are simulated.
256 devices in a mesh: dp: 16 (over y, x_lo, core), mp: 16 (over x_hi, z).
Axes of the slice: x: 4 (x_hi: 2, x_lo: 2; x = x_hi * 2 + x_lo), y: 4, z: 8, core: 2. Of those that a mesh axis runs over, the one named last changes fastest.
Arguments:
- token_ids: int32 [32, 16], replicated, may hold values from 0 to 64511
- prompt_lengths: int32 [32], replicated, may hold values from 128 to 6144, as said below
- cache_codes: bfloat16 [32, 6144, 2, 1024], P('dp', 'mp'), may hold values from -1 to 1
- cache_scales: bfloat16 [32, 48, 2, 1024], P('dp', 'mp'), may hold values from 0.03 to 400
- embedding: bfloat16 [64512, 8192], P('mp', 'dp'), may hold values from -12 to 12
- norm_gain: bfloat16 [8192], P('dp'), may hold values from 0.099609375 to 1.8984375
- query_weight: bfloat16 [8192, 8192], P('dp', 'mp'), may hold values from -0.0625 to 0.0625
- key_value_weight: bfloat16 [8192, 2, 1024], P('dp'), may hold values from -0.0625 to 0.0625
- output_weight: bfloat16 [8192, 8192], P('mp', 'dp'), may hold values from -0.0625 to 0.0625
Outputs:
- layer_out: bfloat16 [32, 16, 8192], P(None, None, 'dp')
Inputs may be any that keep to these rules, and one draw needn't show every extreme that they name: `prompt_lengths`: each a multiple of 128; some row has exactly 6144 in every draw.
All inputs are finite; a program needn't handle non-finite values.
Results may differ from a plain program's by a relative error of at most 0.0065.
The roundings to bfloat16 on the way count: a program that leaves them out, or rounds other values in their place, can miss the bound.
Values may be sent and summed in bfloat16 or wider, within the bound.
A program may use at most 128 MiB of HBM per device.

v0:
```python
import math

import jax
import jax.numpy as jnp
from jax import lax
from jax.sharding import PartitionSpec as P

D = 8192
QH = 64
KVH = 8
HEAD = 128
FACTOR_GROUP = 128
NEW = 16


ROPE_BASE = 500000.0
EPSILON = 1e-05
LOWEST = -1e30


def split_up(shard, dim, devices):
    before, after = (shard.shape[:dim], shard.shape[dim + 1 :])
    return jnp.moveaxis(shard.reshape(*before, devices, -1, *after), dim, 0)


def sent_and_summed(shard, axis, dim):
    pieces = split_up(shard, dim, lax.axis_size(axis))
    arrived = lax.all_to_all(pieces, axis, split_axis=0, concat_axis=0, tiled=True)
    return arrived.sum(axis=0)


def rows_for(lines, devices):
    spare = -len(lines) % devices
    return jnp.pad(lines, [(0, spare)] + [(0, 0)] * (lines.ndim - 1))


def joined_along(pieces, dim):
    shape = list(pieces.shape[1:])
    shape[dim] *= pieces.shape[0]
    return jnp.moveaxis(pieces, 0, dim).reshape(shape)


def copy_for_each(shard, axis):
    copies = jnp.broadcast_to(shard, (lax.axis_size(axis), *shard.shape))
    return lax.all_to_all(copies, axis, split_axis=0, concat_axis=0, tiled=True)


def gather_directly(shard, axis, dim):
    return joined_along(copy_for_each(shard, axis), dim)


def total_of(shard, axes):
    lines = shard.reshape(-1, shard.shape[-1])
    own = sent_and_summed(rows_for(lines, lax.axis_size(axes)), axes, 0)
    whole = gather_directly(own, axes, 0)
    return whole[: len(lines)].reshape(shard.shape)


def sent_together(arrays, axis, dim, along):
    ends, at = ([], 0)
    for a in arrays[:-1]:
        at += a.shape[along]
        ends.append(at)
    both = jnp.concatenate(arrays, axis=along)
    return tuple(jnp.split(lax.all_gather(both, axis, axis=dim, tiled=True), ends, axis=along))


def collected_together(shard, axis):
    leaves = jax.tree.leaves(shard)
    order = sorted(range(len(leaves)), key=lambda k: -leaves[k].size)
    width = (1, *leaves[order[0]].shape)[-1]
    lines = [
        jnp.pad(leaves[k].reshape(-1), (0, -leaves[k].size % width)).reshape(-1, width)
        for k in order
    ]
    both, at, found = (copy_for_each(jnp.concatenate(lines), axis), 0, {})
    for k, line in zip(order, lines):
        share = both[:, at : at + len(line)].reshape(len(both), -1)
        found[k] = share[:, : leaves[k].size].reshape(-1, *leaves[k].shape)
        at += len(line)
    numbers = iter(range(len(leaves)))
    return jax.tree.map(lambda _: found[next(numbers)], shard)


def combined_pairwise(pieces, combine):
    while len(jax.tree.leaves(pieces)[0]) > 1:
        pieces = jax.vmap(combine)(
            *(jax.tree.map(lambda part: part[side::2], pieces) for side in (0, 1))
        )
    return jax.tree.map(lambda part: part[0], pieces)


def joined_all(shard, axis, combine):
    pieces = collected_together(shard, axis)
    return combined_pairwise(pieces, combine)


def sent_together_2(arrays, axis, dim, along):
    widths = [math.prod(a.shape[along:]) for a in arrays]
    both = jnp.concatenate(
        [a.reshape(*a.shape[:along], w) for a, w in zip(arrays, widths)], axis=along
    )
    whole = lax.psum_scatter(both, axis, scatter_dimension=dim, tiled=True)
    pieces = jnp.split(whole, [sum(widths[:k]) for k in range(1, len(widths))], axis=along)
    return tuple(
        (b.reshape(*whole.shape[:along], *a.shape[along:]) for a, b in zip(arrays, pieces))
    )


def rotate(values, positions):
    width = values.shape[-1]
    half_width = width // 2
    exponent = jnp.arange(half_width, dtype=jnp.float32) * (2.0 / width)
    rates = jnp.exp(-jnp.log(ROPE_BASE) * exponent)
    angles = positions[..., None].astype(jnp.float32) * rates
    cosine = jnp.cos(angles)
    sinus_term = jnp.sin(angles)
    first = values[..., :half_width]
    second = values[..., half_width:]
    return jnp.concatenate(
        [first * cosine - second * sinus_term, second * cosine + first * sinus_term], axis=-1
    )


def tensor_total(partial_value):
    return total_of(partial_value, "mp")


def combine_totals(earlier, later):
    largest = jnp.maximum(earlier[0], later[0])
    return (
        largest,
        earlier[1] * jnp.exp(earlier[0] - largest) + later[1] * jnp.exp(later[0] - largest),
    )


def attend_in_place(queries, new_keys, new_values, cache_codes, cache_scales, lengths, place):
    rows_local = queries.shape[0]
    whole_queries, whole_keys, whole_values = (
        lax.all_gather(queries, "mp", axis=2, tiled=True),
        *sent_together((new_keys, new_values), "mp", 2, 0),
    )
    pair = whole_keys.shape[2] // KVH
    whole_keys = whole_keys.reshape(rows_local, NEW, KVH, pair, HEAD)[:, :, :, 0]
    whole_values = whole_values.reshape(rows_local, NEW, KVH, pair, HEAD)[:, :, :, 0]
    grouped = whole_queries.reshape(rows_local, NEW, KVH, QH // KVH, HEAD)
    span = cache_codes.shape[1]
    widened = cache_codes.astype(jnp.float32).reshape(
        rows_local, span // FACTOR_GROUP, FACTOR_GROUP, 2, KVH * HEAD
    )
    block_scales = cache_scales.astype(jnp.float32).reshape(
        rows_local, span // FACTOR_GROUP, 1, 2, KVH * HEAD
    )
    cache = (widened * block_scales).astype(jnp.bfloat16).reshape(rows_local, span, 2, KVH, HEAD)
    factor = HEAD ** (-0.5)
    older = (
        jnp.einsum("rtkgd,rskd->rkgts", grouped, cache[:, :, 0], preferred_element_type=jnp.float32)
        * factor
    )
    fresh = (
        jnp.einsum("rtkgd,rukd->rkgtu", grouped, whole_keys, preferred_element_type=jnp.float32)
        * factor
    )
    slots = place * span + jnp.arange(span, dtype=jnp.int32)
    older_allowed = (slots[None, :] < lengths[:, None])[:, None, None, None, :]
    steps = jnp.arange(NEW, dtype=jnp.int32)
    fresh_allowed = (steps[None, :] <= steps[:, None]) & (place == 0)
    older = jnp.where(older_allowed, older, -jnp.inf)
    fresh = jnp.where(fresh_allowed, fresh, -jnp.inf)
    top = jnp.maximum(jnp.maximum(jnp.max(older, axis=-1), jnp.max(fresh, axis=-1)), LOWEST)[
        ..., None
    ]
    total = jnp.sum(jnp.exp(older - top), axis=-1, keepdims=True) + jnp.sum(
        jnp.exp(fresh - top), axis=-1, keepdims=True
    )
    largest, whole_total = joined_all((top, total), "mp", combine_totals)
    older_weights = (jnp.exp(older - largest) / whole_total).astype(jnp.bfloat16)
    fresh_weights = (jnp.exp(fresh - largest) / whole_total).astype(jnp.bfloat16)
    partial_value = jnp.einsum(
        "rkgts,rskd->rtkgd", older_weights, cache[:, :, 1], preferred_element_type=jnp.float32
    )
    partial_value = partial_value + jnp.einsum(
        "rkgtu,rukd->rtkgd", fresh_weights, whole_values, preferred_element_type=jnp.float32
    )
    partial_value = partial_value.reshape(rows_local, NEW, QH, HEAD)
    summed = sent_and_summed(partial_value, "mp", 2)
    return summed.astype(jnp.bfloat16)


def on_device(
    token_ids,
    prompt_lengths,
    cache_codes,
    cache_scales,
    embedding,
    norm_gain,
    query_weight,
    key_value_weight,
    output_weight,
):
    parts = lax.axis_size("mp")
    place = lax.axis_index("mp")
    batch_index = lax.axis_index("dp")
    pair = max(parts // KVH, 1)
    per_device = max(KVH // parts, 1)
    rows_local = cache_codes.shape[0]
    vocab_local = embedding.shape[0]
    local_heads = query_weight.shape[1] // HEAD
    local_ids = token_ids.reshape(-1) - place * vocab_local
    inside = (local_ids >= 0) & (local_ids < vocab_local)
    picked = jnp.take(embedding, jnp.clip(local_ids, 0, vocab_local - 1), axis=0)
    embedded = tensor_total(jnp.where(inside[:, None], picked.astype(jnp.float32), 0.0))
    scaled = (embedded * norm_gain.astype(jnp.float32)).astype(jnp.bfloat16)
    squares = jnp.sum(embedded * embedded, axis=1)
    first_head = place // pair * per_device
    weight_slice = lax.dynamic_slice_in_dim(
        key_value_weight, first_head * HEAD, per_device * HEAD, axis=2
    )
    weight_slice = weight_slice.reshape(weight_slice.shape[0], 2 * per_device * HEAD)
    query_part = jnp.dot(scaled, query_weight, preferred_element_type=jnp.float32)
    fresh_part = jnp.dot(scaled, weight_slice, preferred_element_type=jnp.float32)
    query_sum, fresh_sum, square_sum = sent_together_2(
        (query_part, fresh_part, squares), "dp", 0, 1
    )
    inverse = lax.rsqrt(square_sum / D + EPSILON)[:, None]
    lengths = lax.dynamic_slice_in_dim(prompt_lengths, batch_index * rows_local, rows_local)
    positions = (lengths[:, None] + jnp.arange(NEW, dtype=jnp.int32)[None, :])[:, :, None]
    queries = rotate(
        (query_sum * inverse).reshape(rows_local, NEW, local_heads, HEAD), positions
    ).astype(jnp.bfloat16)
    fresh = (fresh_sum * inverse).reshape(rows_local, NEW, 2, per_device, HEAD)
    new_keys = rotate(fresh[:, :, 0], positions).astype(jnp.bfloat16)
    new_values = fresh[:, :, 1].astype(jnp.bfloat16)
    mixed = attend_in_place(
        queries, new_keys, new_values, cache_codes, cache_scales, lengths, place
    )
    mixed = mixed.reshape(rows_local * NEW, local_heads * HEAD)
    partial_value = jnp.dot(
        gather_directly(mixed, "dp", 0), output_weight, preferred_element_type=jnp.float32
    )
    result = tensor_total(partial_value).astype(jnp.bfloat16)
    return result.reshape(token_ids.shape[0], token_ids.shape[1], output_weight.shape[1])


def solution(mesh):
    return jax.shard_map(
        on_device,
        mesh=mesh,
        in_specs=(
            P(),
            P(),
            P("dp", "mp", None, None),
            P("dp", "mp", None, None),
            P("mp", "dp"),
            P("dp"),
            P("dp", "mp"),
            P("dp", None, None),
            P("mp", "dp"),
        ),
        out_specs=P(None, None, "dp"),
        check_vma=False,
    )
```

profile of v0, /device:TPU:2, one launch (start us, length us, event | category | flops | bytes accessed | tf_op | source)
XLA Modules:
  0.0 366.9 jit_solution(13847323160019481383)
XLA Ops:
  8.5 4.7 %gather_fusion = bf16[512,512]{1,0:T(8,128)(2,1)S(1)} fusion(bf16[4032,512]{1,0:T(8,128)(2,1)} %param.13, s32[1024]{0:T(1024)S(1)} %pad_clamp_fusion), kind=kCustom, calls=%fused_computation | custom fusion | bytes 1050624 | tf_op jit(solution)/shard_map/jit(_take)/gather | solution.py:211
  13.5 38.3 %all_to_all.35 = f32[16,32,512]{2,1,0:T(8,128)S(1)} all-to-all(f32[16,32,512]{2,1,0:T(8,128)S(1)} %convert_select_fusion), channel_id=1, replica_groups=mesh['dp'=16,'mp'=16] {'mp'}, dimensions={0} | all-to-all | bytes 2097152 | tf_op jit(solution)/shard_map/all_to_all | solution.py:28
  51.9 1.1 broadcast_in_dim.74
  53.0 4.6 %all-to-all-start.1 = ((f32[16,32,512]{2,1,0:T(8,128)}), f32[16,32,512]{2,1,0:T(8,128)S(1)}, u32[]{:S(2)}, u32[]{:S(2)}) async-start(f32[16,32,512]{2,1,0:T(8,128)} %broadcast_in_dim.74), calls=%async_computation.1 | async-start | bytes 2097152 | tf_op jit(solution)/shard_map/all_to_all | solution.py:45
  57.9 27.4 %all-to-all-done.1 = f32[16,32,512]{2,1,0:T(8,128)S(1)} async-done(((f32[16,32,512]{2,1,0:T(8,128)}), f32[16,32,512]{2,1,0:T(8,128)S(1)}, u32[]{:S(2)}, u32[]{:S(2)}) %all-to-all-start.1) | async-done | bytes 1048608 | tf_op jit(solution)/shard_map/all_to_all | solution.py:45
  86.7 1.7 copy.140
  89.2 4.2 %copy.151 = f32[192,8,8,128]{3,2,1,0:T(8,128)} copy(f32[192,8,8,128]{3,1,2,0:T(8,128)S(1)} %bitcast.116) | data formatting | bytes 12582912
  93.4 8.8 %copy.112 = bf16[2,384,2,1024]{1,3,2,0:T(8,128)(2,1)} copy(bf16[2,384,2,1024]{3,2,1,0:T(2,128)(2,1)} %param.11) | data formatting | bytes 6291456 | tf_op args[2]
  102.2 5.4 %copy.114 = f32[2,384,2,8,128]{4,1,3,0,2:T(8,128)} copy(bf16[2,384,2,8,128]{1,4,3,2,0:T(8,128)(2,1)} %bitcast.118) | data formatting | bytes 9437184 | tf_op jit(solution)/shard_map/reshape | solution.py:148
  108.0 7.9 %fusion = bf16[2,384,2,8,128]{4,1,3,0,2:T(8,128)(2,1)} fusion(f32[2,384,2,8,128]{4,1,3,0,2:T(8,128)} %copy.114, f32[2,384,2,8,128]{4,3,1,2,0:T(8,128)} %bitcast.117), kind=kLoop, calls=%fused_computation.2 | loop fusion | flops 3145728 | bytes 15728640 | tf_op jit(solution)/shard_map/convert_element_type | solution.py:154
  115.9 33.1 %reduce-scatter.4.cloned.1.call-done = f32[32,769]{1,0:T(8,128)} async-done(((f32[512,769]{1,0:T(8,128)}), f32[32,769]{1,0:T(8,128)}) %reduce-scatter.4.cloned.1.call-update) | async-done | bytes 98448 | tf_op jit(solution)/shard_map/reduce_scatter | solution.py:103
  150.9 42.0 %all_gather.7 = bf16[4,16,16,128]{3,1,0,2:T(8,128)(2,1)S(1)} all-gather(bf16[4,16,1,128]{3,1,0,2:T(8,128)(2,1)S(1)} %pad_maximum_fusion.2), channel_id=1, replica_groups=mesh['dp'=16,'mp'=16] {'mp'}, dimensions={2}, use_global_device_ids=true | all-gather | bytes 278528 | tf_op jit(solution)/shard_map/all_gather | solution.py:65
  194.1 38.7 %all_gather.6 = bf16[2,16,64,128]{3,1,0,2:T(8,128)(2,1)S(1)} all-gather(bf16[2,16,4,128]{3,1,0,2:T(8,128)(2,1)S(1)} %copy.120), channel_id=1, replica_groups=mesh['dp'=16,'mp'=16] {'mp'}, dimensions={2}, use_global_device_ids=true | all-gather | bytes 557056 | tf_op jit(solution)/shard_map/all_gather | solution.py:140
  232.8 1.4 fusion.34
  234.2 2.5 bitcast_reduce_fusion
  237.1 2.8 fusion.2
  241.0 4.3 %all-to-all-start.2 = ((f32[16,4096,1]{1,2,0:T(1,128)}), f32[16,4096,1]{1,2,0:T(1,128)S(1)}, u32[]{:S(2)}, u32[]{:S(2)}) async-start(f32[16,4096,1]{1,2,0:T(1,128)} %broadcast_in_dim.78), calls=%async_computation.2 | async-start | bytes 524288 | tf_op jit(solution)/shard_map/all_to_all | solution.py:45
  245.3 11.1 %all-to-all-done.2 = f32[16,4096,1]{1,2,0:T(1,128)S(1)} async-done(((f32[16,4096,1]{1,2,0:T(1,128)}), f32[16,4096,1]{1,2,0:T(1,128)S(1)}, u32[]{:S(2)}, u32[]{:S(2)}) %all-to-all-start.2) | async-done | bytes 262176 | tf_op jit(solution)/shard_map/all_to_all | solution.py:45
  258.3 1.5 copy-done.2
  259.8 2.2 fusion.7
  262.5 24.7 %all_to_all.36 = f32[16,2,16,4,128]{4,2,3,1,0:T(8,128)S(1)} all-to-all(f32[16,2,16,4,128]{4,2,3,1,0:T(8,128)S(1)} %bitcast.121), channel_id=1, replica_groups=mesh['dp'=16,'mp'=16] {'mp'}, dimensions={0} | all-to-all | bytes 2097152 | tf_op jit(solution)/shard_map/all_to_all | solution.py:28
  287.3 17.1 %all_to_all.37 = bf16[16,32,512]{2,1,0:T(8,128)(2,1)S(1)} all-to-all(bf16[16,32,512]{2,1,0:T(8,128)(2,1)S(1)} %broadcast_in_dim.79), channel_id=1, replica_groups=mesh['dp'=16,'mp'=16] {'dp'}, dimensions={0} | all-to-all | bytes 1048576 | tf_op jit(solution)/shard_map/all_to_all | solution.py:45
  304.9 32.5 %all_to_all.38 = f32[16,32,512]{2,1,0:T(8,128)S(1)} all-to-all(f32[16,32,512]{2,1,0:T(8,128)S(1)} %fusion.13), channel_id=1, replica_groups=mesh['dp'=16,'mp'=16] {'mp'}, dimensions={0} | all-to-all | bytes 2097152 | tf_op jit(solution)/shard_map/all_to_all | solution.py:28
  337.5 21.8 %all_to_all.39 = bf16[16,32,512]{2,1,0:T(8,128)(2,1)S(1)} all-to-all(bf16[16,32,512]{2,1,0:T(8,128)(2,1)S(1)} %broadcast_in_dim.80), channel_id=1, replica_groups=mesh['dp'=16,'mp'=16] {'mp'}, dimensions={0} | all-to-all | bytes 1048576 | tf_op jit(solution)/shard_map/all_to_all | solution.py:45
  (90 shorter events, 13.4 us)
Async XLA Ops:
  6.5 51.1 %copy-start = (bf16[512,2,1024]{2,1,0:T(2,128)(2,1)S(1)}, bf16[512,2,1024]{2,1,0:T(2,128)(2,1)}, u32[]{:S(2)}) copy-start(bf16[512,2,1024]{2,1,0:T(2,128)(2,1)} %param.16) | copy-start | bytes 6291460
  13.4 44.2 %copy-start.7 = (bf16[512]{0:T(512)(128)(2,1)S(1)}, bf16[512]{0:T(512)(128)(2,1)}, u32[]{:S(2)}) copy-start(bf16[512]{0:T(512)(128)(2,1)} %param.14) | copy-start | bytes 3076
  53.0 32.3 %all-to-all-start.1 = ((f32[16,32,512]{2,1,0:T(8,128)}), f32[16,32,512]{2,1,0:T(8,128)S(1)}, u32[]{:S(2)}, u32[]{:S(2)}) async-start(f32[16,32,512]{2,1,0:T(8,128)} %broadcast_in_dim.74), calls=%async_computation.1 | async-start | bytes 2097152 | tf_op jit(solution)/shard_map/all_to_all | solution.py:45
  57.6 91.4 %reduce-scatter.4.cloned.1.call-start = ((), (), s32[]{:S(2)}) async-start(), calls=%async_computation.8 | async-start | bytes 1949696 | tf_op jit(solution)/shard_map/reduce_scatter | solution.py:103
  57.9 28.2 %copy-start.4 = (bf16[512,512]{1,0:T(8,128)(2,1)S(1)}, bf16[512,512]{1,0:T(8,128)(2,1)}, u32[]{:S(2)}) copy-start(bf16[512,512]{1,0:T(8,128)(2,1)} %param.15) | copy-start | bytes 1572868
  86.7 1.7 copy-start.6
  102.2 5.4 %copy-start.8 = (s32[32]{0:T(128)S(1)}, s32[32]{0:T(128)}, u32[]{:S(2)}) copy-start(s32[32]{0:T(128)} %param.10) | copy-start | bytes 388
  193.9 40.3 %copy-start.3 = (bf16[2,384,2,8,128]{4,1,3,0,2:T(8,128)(2,1)S(1)}, bf16[2,384,2,8,128]{4,1,3,0,2:T(8,128)(2,1)}, u32[]{:S(2)}) copy-start(bf16[2,384,2,8,128]{4,1,3,0,2:T(8,128)(2,1)} %fusion) | copy-start | bytes 9437188
  241.0 15.5 %all-to-all-start.2 = ((f32[16,4096,1]{1,2,0:T(1,128)}), f32[16,4096,1]{1,2,0:T(1,128)S(1)}, u32[]{:S(2)}, u32[]{:S(2)}) async-start(f32[16,4096,1]{1,2,0:T(1,128)} %broadcast_in_dim.78), calls=%async_computation.2 | async-start | bytes 524288 | tf_op jit(solution)/shard_map/all_to_all | solution.py:45
  257.9 1.9 copy-start.2
  262.4 42.0 %copy-start.5 = (bf16[512,512]{1,0:T(8,128)(2,1)S(1)}, bf16[512,512]{1,0:T(8,128)(2,1)}, u32[]{:S(2)}) copy-start(bf16[512,512]{1,0:T(8,128)(2,1)} %param.17) | copy-start | bytes 1572868
  304.5 55.6 %copy-start.1 = (bf16[512,2,1024]{2,1,0:T(2,128)(2,1)S(1)}, bf16[512,2,1024]{2,1,0:T(2,128)(2,1)}, u32[]{:S(2)}) copy-start(bf16[512,2,1024]{2,1,0:T(2,128)(2,1)} %param.16) | copy-start | bytes 6291460
Sparse Core Ops, SparseCore 0:
  88.5 60.4 reduce-scatter.3
where the time goes:
time: 368 us; the launch traced here: 367 us
  blocking collectives  215 us (58%)
  waiting for transfers between devices  71.7 us (19%)
  local copies, waits for them, and re-layouts  32.6 us (9%)
  other arithmetic  17.1 us (5%)
  between operations  13.9 us (4%)
  starting transfers between devices  8.95 us (2%)
  matrix products  7.7 us (2%)
    all_to_all x3, blocking collectives, sent_and_summed(): lax.all_to_all(pieces, axis, split_axis=0, concat_axis=0, tiled=True)  95.5 us
    all_gather x1, blocking collectives, sent_together(): lax.all_gather(both, axis, axis=dim, tiled=True)  42 us
    all_to_all x2, blocking collectives, copy_for_each(): return lax.all_to_all(copies, axis, split_axis=0, concat_axis=0, tiled=True)  38.9 us
    all_gather x1, blocking collectives, attend_in_place(): lax.all_gather(queries, 'mp', axis=2, tiled=True)  38.7 us
    all_to_all x2, waiting for transfers between devices, copy_for_each(): return lax.all_to_all(copies, axis, split_axis=0, concat_axis=0, tiled=True)  38.6 us
    reduce_scatter x1, waiting for transfers between devices, sent_together_2(): whole = lax.psum_scatter(both, axis, scatter_dimension=dim, tiled=True)  33.1 us
    unnamed x27, local copies, waits for them, and re-layouts  17.1 us
    all_to_all x2, starting transfers between devices, copy_for_each(): return lax.all_to_all(copies, axis, split_axis=0, concat_axis=0, tiled=True)  8.9 us
  transfers between devices with their start and end apart: 3, of which 3 were waited for; matrix products, arithmetic and copies ran while one was open for 8% of the time, Pallas kernels for 0%

commit v1 on v0

v1 whole, which is shorter than its diff:
```python
import functools

import jax
import jax.numpy as jnp
from jax import lax
from jax.experimental import pallas as pl
from jax.experimental.pallas import tpu as pltpu
from jax.sharding import PartitionSpec as P

HEAD = 128
FACTOR_GROUP = 128
NEW = 16
ROPE_BASE = 500000.0
EPSILON = 1e-05
LOWEST = -1e30
MESH = pl.DeviceIdType.MESH
BF16 = jnp.bfloat16
F32 = jnp.float32

EMB_RS, EMB_AG, QKV_RS, QKV_AG, MIX_RS, STAT_RS, MIX_AG, OUT_RS, OUT_AG = range(9)


def dot(a, b):
    return jnp.dot(a, b, preferred_element_type=F32)


def dot_last(a, b):
    return lax.dot_general(a, b, (((1,), (1,)), ((), ())), preferred_element_type=F32)


def layer_kernel(
    nd, nm, width,
    lens_ref, ids_ref, table_ref, gain_ref, wkv_ref, scales_ref,
    codes_hbm, emb_hbm, wq_hbm, wo_hbm,
    out_hbm,
    emb, onehot, idsb, codes, wide, keys, valuesT, wq, wo,
    look, look_in, embedded, part, part_in, heads, mix, mix_in, stat, stat_in, mixed,
    outp, outp_in, final,
    send_sem, recv_sem, load_sem, store_sem,
):
    d, m = lax.axis_index("dp"), lax.axis_index("mp")
    groups = 2
    vocab = emb_hbm.shape[0]
    tokens = nd * NEW
    kvh = nm // 2
    span = codes_hbm.shape[1]
    blocks = span // FACTOR_GROUP
    lane = lambda shape: lax.broadcasted_iota(jnp.int32, shape, len(shape) - 1)

    def peer(axis, i):
        if axis == "mp":
            return (d, lax.rem(m + i, nm))
        return (lax.rem(d + i, nd), m)

    def me_of(axis):
        return (m, nm) if axis == "mp" else (d, nd)

    barrier = pltpu.get_barrier_semaphore()
    for axis in ("mp", "dp"):
        def hello(i, c, axis=axis):
            pl.semaphore_signal(barrier, inc=1, device_id=peer(axis, i), device_id_type=MESH)
            return c
        lax.fori_loop(1, me_of(axis)[1], hello, 0)

    chunk = vocab // 4
    loads = [
        pltpu.make_async_copy(
            emb_hbm.at[pl.ds(c * chunk, chunk)], emb.at[pl.ds(c * chunk, chunk)], load_sem.at[c]
        )
        for c in range(4)
    ]
    loads.append(pltpu.make_async_copy(wq_hbm, wq, load_sem.at[4]))
    loads.append(pltpu.make_async_copy(wo_hbm, wo, load_sem.at[5]))
    code_loads = [
        pltpu.make_async_copy(
            codes_hbm.at[g, :, :, pl.ds(k * HEAD, HEAD)], codes.at[g, k], load_sem.at[6 + g * kvh + k]
        )
        for g in range(groups)
        for k in range(kvh)
    ]
    for copy in loads + code_loads:
        copy.start()

    def scatter_copy(ph, g, axis, src, dst, i):
        me, n = me_of(axis)
        dest = lax.rem(me + i, n)
        return pltpu.make_async_remote_copy(
            src_ref=src.at[g, dest], dst_ref=dst.at[g, i - 1],
            send_sem=send_sem.at[0 if ph != STAT_RS else 1, g, i - 1],
            recv_sem=recv_sem.at[ph, g, i - 1],
            device_id=peer(axis, i), device_id_type=MESH,
        )

    def gather_copy(ph, g, axis, buf, i, at):
        return pltpu.make_async_remote_copy(
            src_ref=buf.at[g, at], dst_ref=buf.at[g, at],
            send_sem=send_sem.at[0, g, i - 1], recv_sem=recv_sem.at[ph, g, i - 1],
            device_id=peer(axis, i), device_id_type=MESH,
        )

    def scatter_start(ph, g, axis, src, dst):
        def go(i, c):
            scatter_copy(ph, g, axis, src, dst, i).start()
            return c
        lax.fori_loop(1, me_of(axis)[1], go, 0)

    def scatter_wait(ph, g, axis, src, dst):
        def go(i, c):
            scatter_copy(ph, g, axis, src, dst, i).wait()
            return c
        lax.fori_loop(1, me_of(axis)[1], go, 0)

    def gather_start(ph, g, axis, buf):
        me, n = me_of(axis)
        def go(i, c):
            gather_copy(ph, g, axis, buf, i, me).start()
            return c
        lax.fori_loop(1, n, go, 0)

    def gather_wait(ph, g, axis, buf):
        me, n = me_of(axis)
        def go(i, c):
            gather_copy(ph, g, axis, buf, i, me).wait_send()
            gather_copy(ph, g, axis, buf, i, lax.rem(me + n - i, n)).wait_recv()
            return c
        lax.fori_loop(1, n, go, 0)

    padded = emb.shape[0]
    if padded > vocab:
        emb[pl.ds(vocab, padded - vocab), :] = jnp.zeros((padded - vocab, emb.shape[1]), BF16)
    base = m * vocab

    def lookup(g):
        for j in range(nd):
            r = 2 * j + g
            idsb[pl.ds(j * NEW, NEW), :] = jnp.broadcast_to(ids_ref[:, r : r + 1] - base, (NEW, 128))

        def build(c, carry):
            for s in range(4):
                at = pl.multiple_of((c * 4 + s) * 128, 128)
                hit = idsb[...] - at == lane((tokens, 128))
                onehot[:, pl.ds(at, 128)] = jnp.where(hit, 1.0, 0.0).astype(BF16)
            return carry
        lax.fori_loop(0, padded // 512, build, 0)

    def look_dot(g):
        look[g] = dot(onehot[...], emb[...]).astype(BF16).reshape(nd, NEW, width)

    lookup(0)
    for c in range(4):
        loads[c].wait()
    look_dot(0)
    pl.semaphore_wait(barrier, nd + nm - 2)
    scatter_start(EMB_RS, 0, "mp", look, look_in)
    lookup(1)
    look_dot(1)
    scatter_start(EMB_RS, 1, "mp", look, look_in)

    def widen(g):
        def one(k, carry):
            wide[...] = codes[g, k].reshape(2 * span, HEAD).astype(F32)
            for b in range(blocks):
                sc = scales_ref[g, b, :, pl.ds(pl.multiple_of(k * HEAD, HEAD), HEAD)].astype(F32)
                rows = pl.ds(b * FACTOR_GROUP, FACTOR_GROUP)
                kk = wide[pl.ds(2 * b * FACTOR_GROUP, FACTOR_GROUP, 2), :] * sc[0:1]
                vv = wide[pl.ds(2 * b * FACTOR_GROUP + 1, FACTOR_GROUP, 2), :] * sc[1:2]
                keys[g, k, rows, :] = kk.astype(BF16)
                valuesT[g, k, :, rows] = vv.T.astype(BF16)
            return carry
        lax.fori_loop(0, kvh, one, 0)

    def emb_sum(g):
        scatter_wait(EMB_RS, g, "mp", look, look_in)
        total = look[g, m].astype(F32)
        for i in range(nm - 1):
            total = total + look_in[g, i].astype(F32)
        embedded[g, m] = total.astype(BF16)
        gather_start(EMB_AG, g, "mp", embedded)

    for copy in code_loads[:kvh]:
        copy.wait()
    widen(0)
    emb_sum(0)
    for copy in code_loads[kvh:]:
        copy.wait()
    emb_sum(1)
    widen(1)
    loads[4].wait()
    loads[5].wait()

    def project(g):
        gather_wait(EMB_AG, g, "mp", embedded)
        x = embedded[g].reshape(tokens, width).astype(F32)
        scaled = (x * gain_ref[...].astype(F32)).astype(BF16)
        square = x * x
        s = square[:, 0:128]
        for c in range(1, width // 128):
            s = s + square[:, c * 128 : (c + 1) * 128]
        s = s.reshape(nd, 2, 8, 128)
        a = s[:, 0].reshape(nd * 8, 128)
        b = s[:, 1].reshape(nd * 8, 128)
        a = a + pltpu.roll(a, 64, 1)
        b = b + pltpu.roll(b, 64, 1)
        part[g, :, 10] = jnp.where(lane(a.shape) < 64, a, b).reshape(nd, 8, 128)
        q = dot(scaled, wq[...])
        for c in range(4):
            part[g, :, 2 * c : 2 * c + 2] = q[:, c * HEAD : (c + 1) * HEAD].reshape(nd, 2, 8, 128)
        part[g, :, 8:10] = dot(scaled, wkv_ref[...]).reshape(nd, 2, 8, 128)
        scatter_start(QKV_RS, g, "dp", part, part_in)

    def rotate_heads(g):
        scatter_wait(QKV_RS, g, "dp", part, part_in)
        total = part[g, d]
        for i in range(nd - 1):
            total = total + part_in[g, i]
        sq = total[10]
        low = lane((8, 128)) < 64
        sums = jnp.concatenate(
            [
                jnp.sum(jnp.where(low, sq, 0.0), axis=1, keepdims=True),
                jnp.sum(jnp.where(low, 0.0, sq), axis=1, keepdims=True),
            ],
            axis=0,
        )
        inverse = lax.rsqrt(sums / (nd * width) + EPSILON)
        cosine, sine = table_ref[g, 0], table_ref[g, 1]
        odd = lax.rem(m, 2) == 1
        for c in range(5):
            v = total[2 * c : 2 * c + 2].reshape(NEW, HEAD) * inverse
            turned = v * cosine + pltpu.roll(v, 64, 1) * sine
            if c == 4:
                turned = jnp.where(odd, v, turned)
            heads[g, m, c] = turned.astype(BF16)
        gather_start(QKV_AG, g, "mp", heads)

    factor = HEAD ** (-0.5)
    half = lane((64, 128)) < 64
    half2 = lane((2, 128)) < 64

    def attend(g):
        gather_wait(QKV_AG, g, "mp", heads)
        live = lens_ref[2 * d + g] - m * span
        allowed = lax.broadcasted_iota(jnp.int32, (span, 128), 0) < live

        def one(k, carry):
            q = heads[g, pl.ds(2 * k, 2), 0:4].reshape(128, HEAD)
            s = jnp.where(allowed, dot_last(keys[g, k], q) * factor, -jnp.inf)
            top = jnp.maximum(jnp.max(s, axis=0, keepdims=True), LOWEST)
            p = jnp.exp(s - top)
            st = jnp.concatenate([top, jnp.sum(p, axis=0, keepdims=True)], axis=0)
            o = dot(valuesT[g, k], p.astype(BF16))
            lo, hi = o[0:64], o[64:128]
            mix[g, 2 * k] = jnp.where(half, lo, pltpu.roll(hi, 64, 1)).astype(BF16)
            mix[g, 2 * k + 1] = jnp.where(half, pltpu.roll(lo, 64, 1), hi).astype(BF16)
            turned = pltpu.roll(st, 64, 1)
            stat[g, 2 * k] = jnp.where(half2, st, turned)
            stat[g, 2 * k + 1] = jnp.where(half2, turned, st)
            return carry
        lax.fori_loop(0, kvh, one, 0)
        scatter_start(STAT_RS, g, "mp", stat, stat_in)
        scatter_start(MIX_RS, g, "mp", mix, mix_in)

    def fresh_part(g):
        pair = 2 * (m // 2)
        q = heads[g, m, 0:4].reshape(64, HEAD)
        q = jnp.concatenate([q, q], axis=0)
        s = dot_last(heads[g, pair, 4], q) * factor
        step = lax.rem(lane((NEW, 128)), NEW)
        s = jnp.where(lax.broadcasted_iota(jnp.int32, (NEW, 128), 0) <= step, s, -jnp.inf)
        top = jnp.max(s, axis=0, keepdims=True)
        p = jnp.exp(s - top)
        o = dot(heads[g, pair + 1, 4].astype(F32).T.astype(BF16), p.astype(BF16))
        return top, jnp.sum(p, axis=0, keepdims=True), jnp.where(half, o[0:64], o[64:128])

    def mix_heads(g):
        top_f, sum_f, o_f = fresh_part(g)
        scatter_wait(STAT_RS, g, "mp", stat, stat_in)
        scatter_wait(MIX_RS, g, "mp", mix, mix_in)
        stats = [stat[g, m]] + [stat_in[g, i] for i in range(nm - 1)]
        largest = top_f
        for st in stats:
            largest = jnp.maximum(largest, st[0:1])
        w = jnp.exp(top_f - largest)
        total = sum_f * w
        acc = o_f * w
        for i, st in enumerate(stats):
            w = jnp.exp(st[0:1] - largest)
            total = total + w * st[1:2]
            o = mix[g, m] if i == 0 else mix_in[g, i - 1]
            acc = acc + w * o.astype(F32)
        acc = acc / total
        full = jnp.concatenate([acc, pltpu.roll(acc, 64, 1)], axis=0)
        mixed[g, d] = full.T[0:64].astype(BF16).reshape(4, NEW, HEAD)
        gather_start(MIX_AG, g, "dp", mixed)

    def out_project(g):
        gather_wait(MIX_AG, g, "dp", mixed)
        a = jnp.concatenate([mixed[g, :, h].reshape(tokens, HEAD) for h in range(4)], axis=1)
        outp[g] = dot(a, wo[...]).astype(BF16).reshape(nd, NEW, width)
        scatter_start(OUT_RS, g, "mp", outp, outp_in)

    def out_sum(g):
        scatter_wait(OUT_RS, g, "mp", outp, outp_in)
        total = outp[g, m].astype(F32)
        for i in range(nm - 1):
            total = total + outp_in[g, i].astype(F32)
        final[g, m] = total.astype(BF16)
        gather_start(OUT_AG, g, "mp", final)

    def finish(g):
        gather_wait(OUT_AG, g, "mp", final)
        return pltpu.make_async_copy(final.at[g], out_hbm.at[:, g], store_sem.at[g])

    for stage in (project, rotate_heads, attend, mix_heads, out_project, out_sum):
        for g in range(groups):
            stage(g)
    stores = []
    for g in range(groups):
        copy = finish(g)
        copy.start()
        stores.append(copy)
    for copy in stores:
        copy.wait()


def on_device(
    token_ids, prompt_lengths, cache_codes, cache_scales, embedding, norm_gain,
    query_weight, key_value_weight, output_weight,
):
    nm, nd = lax.axis_size("mp"), lax.axis_size("dp")
    m, d = lax.axis_index("mp"), lax.axis_index("dp")
    vocab, width = embedding.shape
    rows, span = cache_codes.shape[:2]
    kvh = nm // 2
    padded = -(-vocab // 512) * 512
    tokens = nd * NEW

    wkv = lax.dynamic_slice(
        key_value_weight, (0, lax.rem(m, 2), (m // 2) * HEAD), (width, 1, HEAD)
    ).reshape(width, HEAD)
    lengths = lax.dynamic_slice_in_dim(prompt_lengths, d * rows, rows)
    positions = lengths[:, None] + jnp.arange(NEW, dtype=jnp.int32)[None, :]
    exponent = jnp.arange(HEAD // 2, dtype=F32) * (2.0 / HEAD)
    rates = jnp.exp(-jnp.log(ROPE_BASE) * exponent)
    angles = positions[..., None].astype(F32) * rates
    cosine, sine = jnp.cos(angles), jnp.sin(angles)
    table = jnp.stack(
        [
            jnp.concatenate([cosine, cosine], axis=-1),
            jnp.concatenate([-sine, sine], axis=-1),
        ],
        axis=1,
    )

    vmem = pl.BlockSpec(memory_space=pltpu.VMEM)
    hbm = pl.BlockSpec(memory_space=pl.ANY)
    smem = pl.BlockSpec(memory_space=pltpu.SMEM)
    V = pltpu.VMEM
    out = pl.pallas_call(
        functools.partial(layer_kernel, nd, nm, width),
        out_shape=jax.ShapeDtypeStruct((nd, rows, NEW, width), BF16),
        in_specs=[smem, vmem, vmem, vmem, vmem, vmem, hbm, hbm, hbm, hbm],
        out_specs=hbm,
        scratch_shapes=[
            V((padded, width), BF16),
            V((tokens, padded), BF16),
            V((tokens, 128), jnp.int32),
            V((rows, kvh, span, 2, HEAD), BF16),
            V((2 * span, HEAD), F32),
            V((rows, kvh, span, HEAD), BF16),
            V((rows, kvh, HEAD, span), BF16),
            V(query_weight.shape, BF16),
            V(output_weight.shape, BF16),
            V((rows, nd, NEW, width), BF16),
            V((rows, nm - 1, NEW, width), BF16),
            V((rows, nm, NEW, width), BF16),
            V((rows, nd, 11, 8, 128), F32),
            V((rows, nd - 1, 11, 8, 128), F32),
            V((rows, nm, 5, NEW, HEAD), BF16),
            V((rows, nm, 64, 128), BF16),
            V((rows, nm - 1, 64, 128), BF16),
            V((rows, nm, 2, 128), F32),
            V((rows, nm - 1, 2, 128), F32),
            V((rows, nd, 4, NEW, HEAD), BF16),
            V((rows, nd, NEW, width), BF16),
            V((rows, nm - 1, NEW, width), BF16),
            V((rows, nm, NEW, width), BF16),
            pltpu.SemaphoreType.DMA((2, rows, max(nm, nd) - 1)),
            pltpu.SemaphoreType.DMA((9, rows, max(nm, nd) - 1)),
            pltpu.SemaphoreType.DMA((6 + rows * kvh,)),
            pltpu.SemaphoreType.DMA((rows,)),
        ],
        compiler_params=pltpu.CompilerParams(
            collective_id=0, has_side_effects=True, vmem_limit_bytes=56 * 2**20
        ),
    )(
        prompt_lengths, token_ids.T, table, norm_gain.reshape(1, width), wkv, cache_scales,
        cache_codes, embedding, query_weight, output_weight,
    )
    return out.reshape(nd * rows, NEW, width)


def solution(mesh):
    return jax.shard_map(
        on_device,
        mesh=mesh,
        in_specs=(
            P(),
            P(),
            P("dp", "mp", None, None),
            P("dp", "mp", None, None),
            P("mp", "dp"),
            P("dp"),
            P("dp", "mp"),
            P("dp", None, None),
            P("mp", "dp"),
        ),
        out_specs=P(None, None, "dp"),
        check_vma=False,
    )
```

time: 368 us -> 117 us (0.32)
  blocking collectives: 215 us -> 0 us
  Pallas kernels: 0 us -> 109 us
  waiting for transfers between devices: 71.7 us -> 0 us
  local copies, waits for them, and re-layouts: 32.6 us -> 5.15 us
  other arithmetic: 17.1 us -> 0.93 us
  between operations: 13.9 us -> 0.02 us
  starting transfers between devices: 8.95 us -> 0 us
  matrix products: 7.7 us -> 0 us
    all_to_all x5 -> x0, blocking collectives: 134 us -> none  [the longest x3 95.5 us: sent_and_summed(): lax.all_to_all(pieces, axis, split_axis=0, concat_axis=0, tiled=True)]
    pallas_call x0 -> x1, Pallas kernels: none -> 109 us  [on_device(): pl.pallas_call(functools.partial(layer_kernel, nd, nm, width), out_shape=...]
    all_gather x2 -> x0, blocking collectives: 80.6 us -> none  [the longest x1 42 us: sent_together(): lax.all_gather(both, axis, axis=dim, tiled=True)]
    all_to_all x2 -> x0, waiting for transfers between devices: 38.6 us -> none  [copy_for_each(): return lax.all_to_all(copies, axis, split_axis=0, concat_axis=0, tiled=True)]
    reduce_scatter x1 -> x0, waiting for transfers between devices: 33.1 us -> none  [sent_together_2(): whole = lax.psum_scatter(both, axis, scatter_dimension=dim, tiled=True)]
    unnamed x27 -> x4, local copies, waits for them, and re-layouts: 17.1 us -> 2.55 us
    all_to_all x2 -> x0, starting transfers between devices: 8.9 us -> none  [copy_for_each(): return lax.all_to_all(copies, axis, split_axis=0, concat_axis=0, tiled=True)]
    convert_element_type x5 -> x1, other arithmetic: 8.29 us -> 0.07 us  [on_device(): angles = positions[..., None].astype(F32) * rates]
  transfers between devices with their start and end apart: 3 -> 0, of which waited for: 3 -> 0; matrix products, arithmetic and copies ran while one was open for 8% -> 0% of each run, Pallas kernels for 0% -> 0%
where the time goes in v1:
time: 117 us; the launch traced here: 115 us
  Pallas kernels  109 us (93%)
  local copies, waits for them, and re-layouts  5.15 us (4%)
    pallas_call x1, Pallas kernels, on_device(): pl.pallas_call(functools.partial(layer_kernel, nd, nm, width), out_shape=...  109 us
    unnamed x4, local copies, waits for them, and re-layouts  2.55 us

profile of v1, /device:TPU:2, one launch (start us, length us, event | category | flops | bytes accessed | tf_op | source)
XLA Modules:
  0.0 115.1 jit_solution(2902352085834031270)
XLA Ops:
  0.0 0.0 copy-start
  0.0 0.9 dynamic_slice.6
  0.9 0.1 add_convert_fusion
  1.0 1.3 %reshape.37.gain_ref = bf16[1,512]{1,0:T(2,128)(2,1)} reshape(bf16[512]{0:T(512)(128)(2,1)} %param.14) | data formatting | bytes 2048 | tf_op jit(solution)/shard_map/reshape | solution.py:397
  2.2 0.1 multiply_cosine_fusion
  2.4 0.1 maximum_bitcast_fusion
  2.5 0.6 pad_maximum_fusion.table_ref
  3.1 0.0 copy-done
  3.1 0.5 constant_dynamic-slice_fusion
  3.6 0.7 copy.15
  4.2 109.0 %shard_map.91 = bf16[16,2,16,512]{3,2,1,0:T(8,128)(2,1)} custom-call(s32[32]{0:T(128)} %lens_ref.1, s32[16,32]{1,0:T(8,128)} %bitcast.13, f32[2,2,16,128]{3,2,1,0:T(8,128)} %pad_maximum_fusion.table_ref, bf16[1,512]{1,0:T(2,128)(2,1)} %reshape.37.gain_ref, bf16[512,128]{1,0:T(8,128)(2,1)} %bitcast.12, bf16[2,3,2,1024]{3,2,1,0:T(2,128)(2,1)} %scales_ref.1, ...), custom_call_target="tpu_custom_call" | custom-call | tf_op jit(solution)/shard_map/pallas_call | solution.py:359
  113.2 1.9 %copy.17 = bf16[32,16,512]{2,1,0:T(8,128)(2,1)} copy(bf16[32,16,512]{2,1,0:T(8,128)(2,1)} %bitcast.11) | data formatting | bytes 1048576
  (1 shorter events, 0.0 us)
Async XLA Ops:
  0.0 3.1 %copy-start = (bf16[512,2,1024]{2,1,0:T(2,128)(2,1)S(1)}, bf16[512,2,1024]{2,1,0:T(2,128)(2,1)}, u32[]{:S(2)}) copy-start(bf16[512,2,1024]{2,1,0:T(2,128)(2,1)} %param.16) | copy-start | bytes 6291460

commit v2 on v1

v2 whole, which is shorter than its diff:
```python
import functools

import jax
import jax.numpy as jnp
from jax import lax
from jax.experimental import pallas as pl
from jax.experimental.pallas import tpu as pltpu
from jax.sharding import PartitionSpec as P

HEAD = 128
FACTOR_GROUP = 128
NEW = 16
ROPE_BASE = 500000.0
EPSILON = 1e-05
LOWEST = -1e30
MESH = pl.DeviceIdType.MESH
BF16 = jnp.bfloat16
F32 = jnp.float32

EMB_RS, EMB_AG, CORE_RS, QKV_RS, QKV_AG, KV_SWAP, MIX_RS, STAT_RS, MIX_AG, OUT_RS, OUT_AG = range(11)
SENDERS = {CORE_RS: 1, KV_SWAP: 1, STAT_RS: 2}


def dot(a, b):
    return jnp.dot(a, b, preferred_element_type=F32)


def dot_last(a, b):
    return lax.dot_general(a, b, (((1,), (1,)), ((), ())), preferred_element_type=F32)


def layer_kernel(
    nd, nm, width,
    lens_hbm, ids_hbm, gain_hbm, scales_hbm, codes_hbm, emb_hbm, wq_hbm, wkv_hbm, wo_hbm,
    out_hbm,
    emb, onehot, idsb, codes, wide, keys, valuesT, wq, wkv_in, wkv, wo,
    look, look_x, look_pair, look_in, embedded, part, part_core, part_sum, part_in, heads, fresh,
    mix, mix_in, stat, stat_in, mixed, outp, outp_x, outp_pair, outp_in, final,
    lens_ref, ids_ref, gain_ref, scales_ref,
    send_sem, recv_sem, load_sem, store_sem,
):
    d, m = lax.axis_index("dp"), lax.axis_index("mp")
    groups = 2
    vocab = emb_hbm.shape[0]
    tokens = nd * NEW
    kvh = nm // 2
    nz, nq = nm // 2, nd // 2
    column, z = m // nz, lax.rem(m, nz)
    chip, core = d // 2, lax.rem(d, 2)
    span = codes_hbm.shape[1]
    blocks = span // FACTOR_GROUP
    lane = lambda shape: lax.broadcasted_iota(jnp.int32, shape, len(shape) - 1)

    along_z = lambda i: (d, column * nz + lax.rem(z + i, nz))
    across = (d, (1 - column) * nz + z)
    along_mp = lambda i: (d, lax.rem(m + i, nm))
    along_dp = lambda i: (lax.rem(d + i, nd), m)
    along_chips = lambda i: (2 * lax.rem(chip + i, nq) + core, m)
    other_core = (2 * chip + 1 - core, m)
    kv_partner = (d, 2 * (m // 2) + 1 - lax.rem(m, 2))

    barrier = pltpu.get_barrier_semaphore()
    for along, n in ((along_mp, nm), (along_dp, nd)):
        def hello(i, c, along=along):
            pl.semaphore_signal(barrier, inc=1, device_id=along(i), device_id_type=MESH)
            return c
        lax.fori_loop(1, n, hello, 0)

    n_loads = 7 + groups * kvh
    small = [
        pltpu.make_async_copy(src, dst, load_sem.at[n_loads + i])
        for i, (src, dst) in enumerate(
            ((ids_hbm, ids_ref), (lens_hbm, lens_ref), (gain_hbm, gain_ref), (scales_hbm, scales_ref))
        )
    ]
    chunk = vocab // 4
    loads = [
        pltpu.make_async_copy(
            emb_hbm.at[pl.ds(c * chunk, chunk)], emb.at[pl.ds(c * chunk, chunk)], load_sem.at[c]
        )
        for c in range(4)
    ]
    loads.append(pltpu.make_async_copy(wq_hbm, wq, load_sem.at[4]))
    loads.append(pltpu.make_async_copy(wo_hbm, wo, load_sem.at[5]))
    loads.append(
        pltpu.make_async_copy(
            wkv_hbm.at[:, :, pl.ds(pl.multiple_of((m // 2) * HEAD, HEAD), HEAD)], wkv_in, load_sem.at[6]
        )
    )
    code_loads = [
        pltpu.make_async_copy(
            codes_hbm.at[g, :, :, pl.ds(k * HEAD, HEAD)], codes.at[g, k], load_sem.at[7 + g * kvh + k]
        )
        for g in range(groups)
        for k in range(kvh)
    ]
    for copy in small + loads + code_loads:
        copy.start()

    def remote(ph, g, k, src, dst, device):
        return pltpu.make_async_remote_copy(
            src_ref=src, dst_ref=dst,
            send_sem=send_sem.at[SENDERS.get(ph, 0), g, k], recv_sem=recv_sem.at[ph, g, k],
            device_id=device, device_id_type=MESH,
        )

    def loop(lo, hi, f):
        def body(i, c):
            f(i)
            return c
        lax.fori_loop(lo, hi, body, 0)

    def order(t):
        return nz // 2 + ((t + 1) // 2) * (1 - 2 * lax.rem(t, 2))

    def scatter_copy(ph, g, along, src, dst, dest, i):
        return remote(ph, g, i - 1, src.at[g, dest], dst.at[g, i - 1], along(i))

    def scatter_start(ph, g, along, src, dst, me, n):
        loop(1, n, lambda i: scatter_copy(ph, g, along, src, dst, lax.rem(me + i, n), i).start())

    def scatter_wait(ph, g, along, src, dst, me, n):
        loop(1, n, lambda i: scatter_copy(ph, g, along, src, dst, lax.rem(me + i, n), i).wait())

    def gather_start(ph, g, buf):
        loop(1, nd, lambda i: remote(ph, g, i - 1, buf.at[g, d], buf.at[g, d], along_dp(i)).start())

    def gather_wait(ph, g, buf):
        def go(i):
            remote(ph, g, i - 1, buf.at[g, d], buf.at[g, d], along_dp(i)).wait_send()
            at = lax.rem(d + nd - i, nd)
            remote(ph, g, i - 1, buf.at[g, at], buf.at[g, at], along_dp(i)).wait_recv()
        loop(1, nd, go)

    def z_copy(ph, g, buf, i, at):
        return remote(ph, g, i - 1, buf.at[g, at], buf.at[g, at], along_z(i))

    def x_copy(ph, g, buf, i, at):
        return remote(ph, g, nz - 1 + i, buf.at[g, at], buf.at[g, at], across)

    def behind(i):
        return lax.rem(z + nz - i, nz)

    def spread_start(ph, g, buf):
        loop(0, nz - 1, lambda t: z_copy(ph, g, buf, order(t), m).start())
        x_copy(ph, g, buf, 0, m).start()

    def spread_relay(ph, g, buf):
        def relay(t):
            i = order(t)
            at = column * nz + behind(i)
            z_copy(ph, g, buf, i, at).wait_recv()
            x_copy(ph, g, buf, i, at).start()
        loop(0, nz - 1, relay)

    def spread_wait(ph, g, buf):
        loop(1, nz, lambda i: z_copy(ph, g, buf, i, m).wait_send())
        def done(i):
            x_copy(ph, g, buf, i, column * nz + behind(i)).wait_send()
            x_copy(ph, g, buf, i, (1 - column) * nz + behind(i)).wait_recv()
        loop(0, nz, done)

    def ahead(i):
        return lax.rem(z + i, nz)

    def fold_x(ph, g, src, xin, i):
        return remote(ph, g, nz - 1 + i, src.at[g, (1 - column) * nz + ahead(i)], xin.at[g, i], across)

    def fold_z(ph, g, pair, zin, i):
        return remote(ph, g, i - 1, pair.at[g, i], zin.at[g, i - 1], along_z(i))

    def fold_start(ph, g, src, xin, zin):
        loop(0, nz - 1, lambda t: fold_x(ph, g, src, xin, order(t)).start())
        fold_x(ph, g, src, xin, 0).start()

    def fold_relay(ph, g, src, xin, pair, zin):
        def relay(t):
            i = order(t)
            fold_x(ph, g, src, xin, i).wait()
            pair[g, i] = (src[g, column * nz + ahead(i)].astype(F32) + xin[g, i].astype(F32)).astype(BF16)
            fold_z(ph, g, pair, zin, i).start()
        loop(0, nz - 1, relay)

    def fold_wait(ph, g, src, xin, pair, zin):
        total = src[g, m].astype(F32)
        fold_x(ph, g, src, xin, 0).wait()
        total = total + xin[g, 0].astype(F32)
        loop(1, nz, lambda i: fold_z(ph, g, pair, zin, i).wait())
        for i in range(nz - 1):
            total = total + zin[g, i].astype(F32)
        return total.astype(BF16)

    padded = emb.shape[0]
    if padded > vocab:
        emb[pl.ds(vocab, padded - vocab), :] = jnp.zeros((padded - vocab, emb.shape[1]), BF16)
    base = m * vocab

    def lookup(g):
        for j in range(nd):
            r = 2 * j + g
            idsb[pl.ds(j * NEW, NEW), :] = jnp.broadcast_to(ids_ref[:, r : r + 1] - base, (NEW, 128))

        def build(c, carry):
            for s in range(4):
                at = pl.multiple_of((c * 4 + s) * 128, 128)
                hit = idsb[...] - at == lane((tokens, 128))
                onehot[:, pl.ds(at, 128)] = jnp.where(hit, 1.0, 0.0).astype(BF16)
            return carry
        lax.fori_loop(0, padded // 512, build, 0)

    def look_dot(g):
        look[g] = dot(onehot[...], emb[...]).astype(BF16).reshape(nd, NEW, width)

    small[0].wait()
    lookup(0)
    for c in range(4):
        loads[c].wait()
    look_dot(0)
    pl.semaphore_wait(barrier, nd + nm - 2)
    fold_start(EMB_RS, 0, look, look_x, look_in)
    lookup(1)
    look_dot(1)
    fold_start(EMB_RS, 1, look, look_x, look_in)

    def widen(g):
        def one(k, carry):
            wide[pl.ds(0, 2 * span), :] = codes[g, k].reshape(2 * span, HEAD).astype(F32)
            for b in range(blocks):
                sc = scales_ref[g, b, :, pl.ds(pl.multiple_of(k * HEAD, HEAD), HEAD)].astype(F32)
                rows = pl.ds(b * FACTOR_GROUP, FACTOR_GROUP)
                kk = wide[pl.ds(2 * b * FACTOR_GROUP, FACTOR_GROUP, 2), :] * sc[0:1]
                vv = wide[pl.ds(2 * b * FACTOR_GROUP + 1, FACTOR_GROUP, 2), :] * sc[1:2]
                keys[g, k, rows, :] = kk.astype(BF16)
                valuesT[g, k, :, rows] = vv.T.astype(BF16)
            return carry
        lax.fori_loop(0, kvh, one, 0)

    def emb_sum(g):
        embedded[g, m] = fold_wait(EMB_RS, g, look, look_x, look_pair, look_in)
        spread_start(EMB_AG, g, embedded)

    for copy in small[1:] + code_loads[:kvh]:
        copy.wait()
    widen(0)
    def relays(f, *args):
        return lambda g: f(args[0], g, *args[1:])
    def staged(relay, stage):
        for f in (relay, stage):
            for g in range(groups):
                f(g)
    staged(relays(fold_relay, EMB_RS, look, look_x, look_pair, look_in), emb_sum)
    for copy in code_loads[kvh:]:
        copy.wait()
    widen(1)
    for copy in loads[4:]:
        copy.wait()
    wide[pl.ds(0, 2 * width), :] = wkv_in[...].reshape(2 * width, HEAD).astype(F32)
    odd = lax.rem(m, 2)
    wkv[...] = wide[pl.ds(odd, width, 2), :].astype(BF16)

    half_lane = lax.rem(lane((NEW, HEAD)), HEAD // 2)
    exponent = half_lane.astype(F32) * (2.0 / HEAD)
    rates = jnp.exp(-jnp.log(jnp.full((NEW, HEAD), ROPE_BASE, F32)) * exponent)
    steps = lax.broadcasted_iota(jnp.int32, (NEW, HEAD), 0)
    sign = jnp.where(lane((NEW, HEAD)) < HEAD // 2, -1.0, 1.0)
    tables = []
    for g in range(groups):
        angles = (lens_ref[2 * d + g] + steps).astype(F32) * rates
        tables.append((jnp.cos(angles), jnp.sin(angles) * sign))

    def project(g):
        spread_wait(EMB_AG, g, embedded)
        x = embedded[g].reshape(tokens, width).astype(F32)
        scaled = (x * gain_ref[...].astype(F32).reshape(1, width)).astype(BF16)
        square = x * x
        s = square[:, 0:128]
        for c in range(1, width // 128):
            s = s + square[:, c * 128 : (c + 1) * 128]
        s = s.reshape(nd, 2, 8, 128)
        a = s[:, 0].reshape(nd * 8, 128)
        b = s[:, 1].reshape(nd * 8, 128)
        a = a + pltpu.roll(a, 64, 1)
        b = b + pltpu.roll(b, 64, 1)
        s = jnp.where(lane(a.shape) < 64, a, b).reshape(nq, 2, 8, 128)
        q = dot(scaled, wq[...])
        kv = dot(scaled, wkv[...]).reshape(nq, 2, 2, 8, 128)
        q = [q[:, c * HEAD : (c + 1) * HEAD].reshape(nq, 2, 2, 8, 128) for c in range(4)] + [kv]
        for e in range(2):
            for c in range(5):
                part[g, e, :, 2 * c : 2 * c + 2] = q[c][:, e]
            part[g, e, :, 10] = s[:, e]
        core_copy(g).start()

    def core_copy(g):
        return remote(CORE_RS, g, 0, part.at[g, 1 - core], part_core.at[g], other_core)

    def join_cores(g):
        core_copy(g).wait()
        part_sum[g] = part[g, core] + part_core[g]
        scatter_start(QKV_RS, g, along_chips, part_sum, part_in, chip, nq)

    def kv_copy(g, at):
        return remote(KV_SWAP, g, 1, fresh.at[g, at], fresh.at[g, at], kv_partner)

    def rotate_heads(g):
        scatter_wait(QKV_RS, g, along_chips, part_sum, part_in, chip, nq)
        total = part_sum[g, chip]
        for i in range(nq - 1):
            total = total + part_in[g, i]
        sq = total[10]
        low = lane((8, 128)) < 64
        sums = jnp.concatenate(
            [
                jnp.sum(jnp.where(low, sq, 0.0), axis=1, keepdims=True),
                jnp.sum(jnp.where(low, 0.0, sq), axis=1, keepdims=True),
            ],
            axis=0,
        )
        inverse = lax.rsqrt(sums / (nd * width) + EPSILON)
        cosine, sine = tables[g]
        for c in range(5):
            v = total[2 * c : 2 * c + 2].reshape(NEW, HEAD) * inverse
            turned = v * cosine + pltpu.roll(v, 64, 1) * sine
            if c < 4:
                heads[g, m, c] = turned.astype(BF16)
            else:
                fresh[g, odd] = jnp.where(odd == 1, v, turned).astype(BF16)
        spread_start(QKV_AG, g, heads)
        kv_copy(g, odd).start()

    factor = HEAD ** (-0.5)
    half = lane((64, 128)) < 64
    half2 = lane((2, 128)) < 64

    def attend(g):
        spread_wait(QKV_AG, g, heads)
        live = lens_ref[2 * d + g] - m * span
        allowed = lax.broadcasted_iota(jnp.int32, (span, 128), 0) < live

        def one(k, carry):
            q = heads[g, pl.ds(2 * k, 2)].reshape(128, HEAD)
            s = jnp.where(allowed, dot_last(keys[g, k], q) * factor, -jnp.inf)
            top = jnp.maximum(jnp.max(s, axis=0, keepdims=True), LOWEST)
            p = jnp.exp(s - top)
            st = jnp.concatenate([top, jnp.sum(p, axis=0, keepdims=True)], axis=0)
            o = dot(valuesT[g, k], p.astype(BF16))
            lo, hi = o[0:64], o[64:128]
            mix[g, 2 * k] = jnp.where(half, lo, pltpu.roll(hi, 64, 1)).astype(BF16)
            mix[g, 2 * k + 1] = jnp.where(half, pltpu.roll(lo, 64, 1), hi).astype(BF16)
            turned = pltpu.roll(st, 64, 1)
            stat[g, 2 * k] = jnp.where(half2, st, turned)
            stat[g, 2 * k + 1] = jnp.where(half2, turned, st)
            return carry
        lax.fori_loop(0, kvh, one, 0)
        scatter_start(STAT_RS, g, along_mp, stat, stat_in, m, nm)
        scatter_start(MIX_RS, g, along_mp, mix, mix_in, m, nm)

    def fresh_part(g):
        kv_copy(g, odd).wait_send()
        kv_copy(g, 1 - odd).wait_recv()
        q = heads[g, m].reshape(64, HEAD)
        q = jnp.concatenate([q, q], axis=0)
        s = dot_last(fresh[g, 0], q) * factor
        step = lax.rem(lane((NEW, 128)), NEW)
        s = jnp.where(lax.broadcasted_iota(jnp.int32, (NEW, 128), 0) <= step, s, -jnp.inf)
        top = jnp.max(s, axis=0, keepdims=True)
        p = jnp.exp(s - top)
        o = dot(fresh[g, 1].astype(F32).T.astype(BF16), p.astype(BF16))
        return top, jnp.sum(p, axis=0, keepdims=True), jnp.where(half, o[0:64], o[64:128])

    def mix_heads(g):
        top_f, sum_f, o_f = fresh_part(g)
        scatter_wait(STAT_RS, g, along_mp, stat, stat_in, m, nm)
        scatter_wait(MIX_RS, g, along_mp, mix, mix_in, m, nm)
        stats = [stat[g, m]] + [stat_in[g, i] for i in range(nm - 1)]
        largest = top_f
        for st in stats:
            largest = jnp.maximum(largest, st[0:1])
        w = jnp.exp(top_f - largest)
        total = sum_f * w
        acc = o_f * w
        for i, st in enumerate(stats):
            w = jnp.exp(st[0:1] - largest)
            total = total + w * st[1:2]
            o = mix[g, m] if i == 0 else mix_in[g, i - 1]
            acc = acc + w * o.astype(F32)
        acc = acc / total
        full = jnp.concatenate([acc, pltpu.roll(acc, 64, 1)], axis=0)
        mixed[g, d] = full.T[0:64].astype(BF16).reshape(4, NEW, HEAD)
        gather_start(MIX_AG, g, mixed)

    def out_project(g):
        gather_wait(MIX_AG, g, mixed)
        a = jnp.concatenate([mixed[g, :, h].reshape(tokens, HEAD) for h in range(4)], axis=1)
        outp[g] = dot(a, wo[...]).astype(BF16).reshape(nd, NEW, width)
        fold_start(OUT_RS, g, outp, outp_x, outp_in)

    def out_sum(g):
        final[g, m] = fold_wait(OUT_RS, g, outp, outp_x, outp_pair, outp_in)
        spread_start(OUT_AG, g, final)

    def finish(g):
        spread_wait(OUT_AG, g, final)
        return pltpu.make_async_copy(final.at[g], out_hbm.at[:, g], store_sem.at[g])

    nothing = lambda g: None
    staged(relays(spread_relay, EMB_AG, embedded), project)
    staged(nothing, join_cores)
    staged(nothing, rotate_heads)
    staged(relays(spread_relay, QKV_AG, heads), attend)
    staged(nothing, mix_heads)
    staged(nothing, out_project)
    staged(relays(fold_relay, OUT_RS, outp, outp_x, outp_pair, outp_in), out_sum)
    spread_relay(OUT_AG, 0, final)
    spread_relay(OUT_AG, 1, final)
    stores = []
    for g in range(groups):
        copy = finish(g)
        copy.start()
        stores.append(copy)
    for copy in stores:
        copy.wait()


def on_device(
    token_ids, prompt_lengths, cache_codes, cache_scales, embedding, norm_gain,
    query_weight, key_value_weight, output_weight,
):
    nm, nd = lax.axis_size("mp"), lax.axis_size("dp")
    vocab, width = embedding.shape
    rows, span = cache_codes.shape[:2]
    kvh = nm // 2
    nz, nq = nm // 2, nd // 2
    padded = -(-vocab // 512) * 512
    tokens = nd * NEW

    hbm = pl.BlockSpec(memory_space=pltpu.HBM)
    V = pltpu.VMEM
    out = pl.pallas_call(
        functools.partial(layer_kernel, nd, nm, width),
        out_shape=jax.ShapeDtypeStruct((nd, rows, NEW, width), BF16),
        in_specs=[hbm] * 9,
        out_specs=pl.BlockSpec(memory_space=pl.ANY),
        scratch_shapes=[
            V((padded, width), BF16),
            V((tokens, padded), BF16),
            V((tokens, 128), jnp.int32),
            V((rows, kvh, span, 2, HEAD), BF16),
            V((2 * max(span, width), HEAD), F32),
            V((rows, kvh, span, HEAD), BF16),
            V((rows, kvh, HEAD, span), BF16),
            V(query_weight.shape, BF16),
            V((width, 2, HEAD), BF16),
            V((width, HEAD), BF16),
            V(output_weight.shape, BF16),
            V((rows, nd, NEW, width), BF16),
            V((rows, nz, NEW, width), BF16),
            V((rows, nz, NEW, width), BF16),
            V((rows, nz - 1, NEW, width), BF16),
            V((rows, nm, NEW, width), BF16),
            V((rows, 2, nq, 11, 8, 128), F32),
            V((rows, nq, 11, 8, 128), F32),
            V((rows, nq, 11, 8, 128), F32),
            V((rows, nq - 1, 11, 8, 128), F32),
            V((rows, nm, 4, NEW, HEAD), BF16),
            V((rows, 2, NEW, HEAD), BF16),
            V((rows, nm, 64, 128), BF16),
            V((rows, nm - 1, 64, 128), BF16),
            V((rows, nm, 2, 128), F32),
            V((rows, nm - 1, 2, 128), F32),
            V((rows, nd, 4, NEW, HEAD), BF16),
            V((rows, nd, NEW, width), BF16),
            V((rows, nz, NEW, width), BF16),
            V((rows, nz, NEW, width), BF16),
            V((rows, nz - 1, NEW, width), BF16),
            V((rows, nm, NEW, width), BF16),
            pltpu.SMEM(prompt_lengths.shape, jnp.int32),
            V((NEW, rows * nd), jnp.int32),
            V(norm_gain.shape, BF16),
            V(cache_scales.shape, BF16),
            pltpu.SemaphoreType.DMA((3, rows, max(nm, nd) - 1)),
            pltpu.SemaphoreType.DMA((11, rows, max(nm, nd) - 1)),
            pltpu.SemaphoreType.DMA((11 + rows * kvh,)),
            pltpu.SemaphoreType.DMA((rows,)),
        ],
        compiler_params=pltpu.CompilerParams(
            collective_id=0, has_side_effects=True, vmem_limit_bytes=56 * 2**20
        ),
    )(
        prompt_lengths, token_ids.T, norm_gain, cache_scales,
        cache_codes, embedding, query_weight, key_value_weight, output_weight,
    )
    return out.reshape(nd * rows, NEW, width)


def solution(mesh):
    return jax.shard_map(
        on_device,
        mesh=mesh,
        in_specs=(
            P(),
            P(),
            P("dp", "mp", None, None),
            P("dp", "mp", None, None),
            P("mp", "dp"),
            P("dp"),
            P("dp", "mp"),
            P("dp", None, None),
            P("mp", "dp"),
        ),
        out_specs=P(None, None, "dp"),
        check_vma=False,
    )
```

time: 117 us -> 102 us (0.87); the launches traced: 115 us -> 102 us
  Pallas kernels: 109 us -> 99.9 us
  local copies, waits for them, and re-layouts: 5.15 us -> 1.87 us
    pallas_call x1, Pallas kernels: 109 us -> 99.9 us  [on_device(): pl.pallas_call(functools.partial(layer_kernel, nd, nm, width), out_shape=...]
    dynamic_slice x2 -> x0, local copies, waits for them, and re-layouts: 1.33 us -> none  [the longest x1 0.88 us: on_device(): lengths = lax.dynamic_slice_in_dim(prompt_lengths, d * rows, rows)]
    reshape x1 -> x0, local copies, waits for them, and re-layouts: 1.28 us -> none  [on_device(): norm_gain.reshape(1, width)]
    unnamed x4 -> x1, local copies, waits for them, and re-layouts: 2.55 us -> 1.87 us
where the time goes in v2:
time: 102 us
  Pallas kernels  99.9 us (98%)
  local copies, waits for them, and re-layouts  1.87 us (2%)
    pallas_call x1, Pallas kernels, on_device(): pl.pallas_call(functools.partial(layer_kernel, nd, nm, width), out_shape=...  99.9 us

profile of v2, /device:TPU:2, one launch (start us, length us, event | category | flops | bytes accessed | tf_op | source)
XLA Modules:
  0.0 101.8 jit_solution(7196333781198864893)
XLA Ops:
  0.0 99.9 %shard_map.91 = bf16[16,2,16,512]{3,2,1,0:T(8,128)(2,1)} custom-call(s32[32]{0:T(128)} %lens_hbm.1, s32[16,32]{1,0:T(8,128)} %bitcast.3, bf16[512]{0:T(512)(128)(2,1)} %gain_hbm.1, bf16[2,3,2,1024]{3,2,1,0:T(2,128)(2,1)} %scales_hbm.1, bf16[2,384,2,1024]{3,2,1,0:T(2,128)(2,1)} %codes_hbm.1, bf16[4032,512]{1,0:T(8,128)(2,1)} %emb_hbm.1, ...), custom_call_target="tpu_custom_call" | custom-call | tf_op jit(solution)/shard_map/pallas_call | solution.py:439
  100.0 1.9 %copy.11 = bf16[32,16,512]{2,1,0:T(8,128)(2,1)} copy(bf16[32,16,512]{2,1,0:T(8,128)(2,1)} %bitcast.2) | data formatting | bytes 1048576

commit v3 on v2

--- a/solution.py
+++ b/solution.py
@@ -35,7 +35,7 @@
     out_hbm,
     emb, onehot, idsb, codes, wide, keys, valuesT, wq, wkv_in, wkv, wo,
     look, look_x, look_pair, look_in, embedded, part, part_core, part_sum, part_in, heads, fresh,
-    mix, mix_in, stat, stat_in, mixed, outp, outp_x, outp_pair, outp_in, final,
+    mix, mix_x, mix_pair, mix_in, stat, stat_x, stat_pair, stat_in, mixed, outp, outp_x, outp_pair, outp_in, final,
     lens_ref, ids_ref, gain_ref, scales_ref,
     send_sem, recv_sem, load_sem, store_sem,
 ):
@@ -53,14 +53,14 @@
 
     along_z = lambda i: (d, column * nz + lax.rem(z + i, nz))
     across = (d, (1 - column) * nz + z)
-    along_mp = lambda i: (d, lax.rem(m + i, nm))
     along_dp = lambda i: (lax.rem(d + i, nd), m)
     along_chips = lambda i: (2 * lax.rem(chip + i, nq) + core, m)
     other_core = (2 * chip + 1 - core, m)
     kv_partner = (d, 2 * (m // 2) + 1 - lax.rem(m, 2))
 
     barrier = pltpu.get_barrier_semaphore()
-    for along, n in ((along_mp, nm), (along_dp, nd)):
+    pl.semaphore_signal(barrier, inc=1, device_id=across, device_id_type=MESH)
+    for along, n in ((along_z, nz), (along_dp, nd)):
         def hello(i, c, along=along):
             pl.semaphore_signal(barrier, inc=1, device_id=along(i), device_id_type=MESH)
             return c
@@ -216,7 +216,7 @@
     for c in range(4):
         loads[c].wait()
     look_dot(0)
-    pl.semaphore_wait(barrier, nd + nm - 2)
+    pl.semaphore_wait(barrier, nd + nz - 1)
     fold_start(EMB_RS, 0, look, look_x, look_in)
     lookup(1)
     look_dot(1)
@@ -351,9 +351,39 @@
             stat[g, 2 * k] = jnp.where(half2, st, turned)
             stat[g, 2 * k + 1] = jnp.where(half2, turned, st)
             return carry
-        lax.fori_loop(0, kvh, one, 0)
-        scatter_start(STAT_RS, g, along_mp, stat, stat_in, m, nm)
-        scatter_start(MIX_RS, g, along_mp, mix, mix_in, m, nm)
+        lax.fori_loop(0, kvh, one, 0, unroll=True)
+        def go(i):
+            merge_x(g, i, MIX_RS).start()
+            merge_x(g, i, STAT_RS).start()
+        loop(0, nz - 1, lambda t: go(order(t)))
+        go(0)
+
+    def merge_x(g, i, ph):
+        src, dst = (mix, mix_x) if ph == MIX_RS else (stat, stat_x)
+        return fold_x(ph, g, src, dst, i)
+
+    def merge_z(g, i, ph):
+        src, dst = (mix_pair, mix_in) if ph == MIX_RS else (stat_pair, stat_in)
+        return fold_z(ph, g, src, dst, i)
+
+    def merge(g, i):
+        merge_x(g, i, STAT_RS).wait()
+        merge_x(g, i, MIX_RS).wait()
+        at = column * nz + ahead(i)
+        a, b = stat[g, at], stat_x[g, i]
+        top = jnp.maximum(a[0:1], b[0:1])
+        wa, wb = jnp.exp(a[0:1] - top), jnp.exp(b[0:1] - top)
+        stat_pair[g, i] = jnp.concatenate([top, wa * a[1:2] + wb * b[1:2]], axis=0)
+        mix_pair[g, i] = (wa * mix[g, at].astype(F32) + wb * mix_x[g, i].astype(F32)).astype(BF16)
+
+    def merge_relay(g):
+        def relay(t):
+            i = order(t)
+            merge(g, i)
+            merge_z(g, i, MIX_RS).start()
+            merge_z(g, i, STAT_RS).start()
+        loop(0, nz - 1, relay)
+        merge(g, 0)
 
     def fresh_part(g):
         kv_copy(g, odd).wait_send()
@@ -370,9 +400,11 @@
 
     def mix_heads(g):
         top_f, sum_f, o_f = fresh_part(g)
-        scatter_wait(STAT_RS, g, along_mp, stat, stat_in, m, nm)
-        scatter_wait(MIX_RS, g, along_mp, mix, mix_in, m, nm)
-        stats = [stat[g, m]] + [stat_in[g, i] for i in range(nm - 1)]
+        def done(i):
+            merge_z(g, i, STAT_RS).wait()
+            merge_z(g, i, MIX_RS).wait()
+        loop(1, nz, done)
+        stats = [stat_pair[g, 0]] + [stat_in[g, i] for i in range(nz - 1)]
         largest = top_f
         for st in stats:
             largest = jnp.maximum(largest, st[0:1])
@@ -382,7 +414,7 @@
         for i, st in enumerate(stats):
             w = jnp.exp(st[0:1] - largest)
             total = total + w * st[1:2]
-            o = mix[g, m] if i == 0 else mix_in[g, i - 1]
+            o = mix_pair[g, 0] if i == 0 else mix_in[g, i - 1]
             acc = acc + w * o.astype(F32)
         acc = acc / total
         full = jnp.concatenate([acc, pltpu.roll(acc, 64, 1)], axis=0)
@@ -408,7 +440,7 @@
     staged(nothing, join_cores)
     staged(nothing, rotate_heads)
     staged(relays(spread_relay, QKV_AG, heads), attend)
-    staged(nothing, mix_heads)
+    staged(merge_relay, mix_heads)
     staged(nothing, out_project)
     staged(relays(fold_relay, OUT_RS, outp, outp_x, outp_pair, outp_in), out_sum)
     spread_relay(OUT_AG, 0, final)
@@ -465,9 +497,13 @@
             V((rows, nm, 4, NEW, HEAD), BF16),
             V((rows, 2, NEW, HEAD), BF16),
             V((rows, nm, 64, 128), BF16),
-            V((rows, nm - 1, 64, 128), BF16),
+            V((rows, nz, 64, 128), BF16),
+            V((rows, nz, 64, 128), BF16),
+            V((rows, nz - 1, 64, 128), BF16),
             V((rows, nm, 2, 128), F32),
-            V((rows, nm - 1, 2, 128), F32),
+            V((rows, nz, 2, 128), F32),
+            V((rows, nz, 2, 128), F32),
+            V((rows, nz - 1, 2, 128), F32),
             V((rows, nd, 4, NEW, HEAD), BF16),
             V((rows, nd, NEW, width), BF16),
             V((rows, nz, NEW, width), BF16),

time: 102 us -> 96.1 us (0.942)
  Pallas kernels: 99.9 us -> 94 us
    pallas_call x1, Pallas kernels: 99.9 us -> 94 us  [on_device(): pl.pallas_call(functools.partial(layer_kernel, nd, nm, width), out_shape=...]
where the time goes in v3:
time: 96.1 us; the launch traced here: 95.9 us
  Pallas kernels  94 us (98%)
  local copies, waits for them, and re-layouts  1.87 us (2%)
    pallas_call x1, Pallas kernels, on_device(): pl.pallas_call(functools.partial(layer_kernel, nd, nm, width), out_shape=...  94 us

profile of v3, /device:TPU:2, one launch (start us, length us, event | category | flops | bytes accessed | tf_op | source)
XLA Modules:
  0.0 95.9 jit_solution(16071991240002417330)
XLA Ops:
  0.0 94.0 %shard_map.91 = bf16[16,2,16,512]{3,2,1,0:T(8,128)(2,1)} custom-call(s32[32]{0:T(128)} %lens_hbm.1, s32[16,32]{1,0:T(8,128)} %bitcast.3, bf16[512]{0:T(512)(128)(2,1)} %gain_hbm.1, bf16[2,3,2,1024]{3,2,1,0:T(2,128)(2,1)} %scales_hbm.1, bf16[2,384,2,1024]{3,2,1,0:T(2,128)(2,1)} %codes_hbm.1, bf16[4032,512]{1,0:T(8,128)(2,1)} %emb_hbm.1, ...), custom_call_target="tpu_custom_call" | custom-call | tf_op jit(solution)/shard_map/pallas_call | solution.py:471
  94.1 1.9 %copy.11 = bf16[32,16,512]{2,1,0:T(8,128)(2,1)} copy(bf16[32,16,512]{2,1,0:T(8,128)(2,1)} %bitcast.2) | data formatting | bytes 1048576

commit v4 on v3

--- a/solution.py
+++ b/solution.py
@@ -142,12 +142,12 @@
         return lax.rem(z + nz - i, nz)
 
     def spread_start(ph, g, buf):
-        loop(0, nz - 1, lambda t: z_copy(ph, g, buf, order(t), m).start())
+        loop(0, nz - 1, lambda t: z_copy(ph, g, buf, order(nz - 2 - t), m).start())
         x_copy(ph, g, buf, 0, m).start()
 
     def spread_relay(ph, g, buf):
         def relay(t):
-            i = order(t)
+            i = order(nz - 2 - t)
             at = column * nz + behind(i)
             z_copy(ph, g, buf, i, at).wait_recv()
             x_copy(ph, g, buf, i, at).start()

time: 96.1 us -> 96 us (level)
  no operation moved by 1% of the time
where the time goes in v4:
time: 96 us; the launch traced here: 95.8 us
  Pallas kernels  94 us (98%)
  local copies, waits for them, and re-layouts  1.87 us (2%)
    pallas_call x1, Pallas kernels, on_device(): pl.pallas_call(functools.partial(layer_kernel, nd, nm, width), out_shape=...  94 us

profile of v4, /device:TPU:2, one launch (start us, length us, event | category | flops | bytes accessed | tf_op | source)
XLA Modules:
  0.0 95.8 jit_solution(1263412937933554396)
XLA Ops:
  0.0 94.0 %shard_map.91 = bf16[16,2,16,512]{3,2,1,0:T(8,128)(2,1)} custom-call(s32[32]{0:T(128)} %lens_hbm.1, s32[16,32]{1,0:T(8,128)} %bitcast.3, bf16[512]{0:T(512)(128)(2,1)} %gain_hbm.1, bf16[2,3,2,1024]{3,2,1,0:T(2,128)(2,1)} %scales_hbm.1, bf16[2,384,2,1024]{3,2,1,0:T(2,128)(2,1)} %codes_hbm.1, bf16[4032,512]{1,0:T(8,128)(2,1)} %emb_hbm.1, ...), custom_call_target="tpu_custom_call" | custom-call | tf_op jit(solution)/shard_map/pallas_call | solution.py:471
  94.0 1.9 %copy.11 = bf16[32,16,512]{2,1,0:T(8,128)(2,1)} copy(bf16[32,16,512]{2,1,0:T(8,128)(2,1)} %bitcast.2) | data formatting | bytes 1048576
